TPU v7x, 128 devices: a whole 4x4x4 slice. The times are simulated.
128 devices in a mesh: dp: 16 (over z, y_lo, core), tensor: 8 (over x, y_hi).
Axes of the slice: x: 4, y: 4 (y_hi: 2, y_lo: 2; y = y_hi * 2 + y_lo), z: 4, core: 2. Of those that a mesh axis runs over, the one named last changes fastest.
Arguments:
- requests: bfloat16 [1024, 8192], P('dp'), may hold values from -6 to 6
- base_gate_up_weight: bfloat16 [8192, 2, 28672], P('dp', None, 'tensor'), may hold values from -0.0625 to 0.0625
- adapter_down_weight: bfloat16 [128, 8192, 128], P('dp', 'tensor'), may hold values from -0.0625 to 0.0625
- adapter_up_weight: bfloat16 [128, 64, 2, 28672], P('dp', None, None, 'tensor'), may hold values from -0.75 to 0.75
- request_adapter: int32 [1024], P('dp'), may hold values from 0 to 127, as said below
- adapter_position: int32 [128], replicated, may hold values from 0 to 127, as said below
- counts: int32 [16], replicated, may hold values from 1 to 64, 768 in all
Outputs:
- hidden: bfloat16 [1024, 28672], P('dp', 'tensor')
Inputs may be any that keep to these rules, and one draw needn't show every extreme that they name: `request_adapter`: the owner of store position s is s // 8. Among the 64 rows of one group at most 8 use adapters of one owner; in every draw one owner receives exactly 8 rows from every group. `adapter_position`: each store position appears once. `counts`: rows of a group past its count are padding.
All inputs are finite; a program needn't handle non-finite values.
Results may differ from a plain program's by a relative error of at most 0.0058.
Values may be sent and summed in bfloat16 or wider, within the bound.
A program may use at most 128 MiB of HBM per device.

v0:
```python
import jax
import jax.numpy as jnp
from jax import lax
from jax.sharding import PartitionSpec as P


def body(
    requests,
    base_gate_up_weight,
    adapter_down_weight,
    adapter_up_weight,
    request_adapter,
    adapter_position,
    counts,
):
    rows = requests.shape[0]
    width = requests.shape[1]
    groups = lax.axis_size("dp")
    lanes = lax.axis_size("tensor")
    holder_adapters = adapter_down_weight.shape[0]
    rank_doubled = adapter_down_weight.shape[2]
    rank_single = rank_doubled // 2
    rank_extent = adapter_up_weight.shape[3]
    capacity = rows // 8
    buffer = groups * capacity
    group = lax.axis_index("dp")
    lane = lax.axis_index("tensor")
    match = (
        request_adapter[:, None] == jnp.arange(adapter_position.shape[0], dtype=jnp.int32)[None, :]
    )
    slot = jnp.sum(jnp.where(match, adapter_position[None, :], 0), axis=1)
    owner = slot // holder_adapters
    local = slot % holder_adapters
    owner_hot = (owner[:, None] == jnp.arange(groups, dtype=jnp.int32)[None, :]).astype(jnp.int32)
    place = jnp.sum(owner_hot * (jnp.cumsum(owner_hot, axis=0) - 1), axis=1)
    target = owner * capacity + place
    select = target[None, :] == jnp.arange(buffer, dtype=jnp.int32)[:, None]
    select_bf = select.astype(jnp.bfloat16)
    width_part = width // lanes
    piece = lax.dynamic_slice_in_dim(requests, lane * width_part, width_part, 1)
    outgoing = jnp.dot(select_bf, piece, preferred_element_type=jnp.float32).astype(jnp.bfloat16)
    row_index = jnp.arange(rows, dtype=jnp.int32)
    labels = jnp.stack(
        [
            jnp.sum(jnp.where(select, local[None, :], 0), axis=1),
            jnp.sum(jnp.where(select, row_index[None, :], 0), axis=1),
        ],
        axis=1,
    ).astype(jnp.bfloat16)
    arrived, arrived_labels = (
        lax.all_to_all(outgoing, "dp", split_axis=0, concat_axis=0, tiled=True),
        lax.all_to_all(labels, "dp", split_axis=0, concat_axis=0, tiled=True),
    )
    which = arrived_labels[:, 0].astype(jnp.int32)
    partial_down = jnp.zeros((buffer, rank_doubled), jnp.float32)
    for adapter_number in range(holder_adapters):
        selected_adapter = jnp.where(
            (which == adapter_number)[:, None], arrived, jnp.zeros_like(arrived)
        )
        partial_down = partial_down + jnp.dot(
            selected_adapter,
            adapter_down_weight[adapter_number],
            preferred_element_type=jnp.float32,
        )
    down = lax.psum(partial_down, "tensor").astype(jnp.bfloat16)
    term_gate = jnp.zeros((buffer, rank_extent), jnp.float32)
    term_up = jnp.zeros((buffer, rank_extent), jnp.float32)
    for adapter_number in range(holder_adapters):
        selected_adapter = jnp.where((which == adapter_number)[:, None], down, jnp.zeros_like(down))
        term_gate = term_gate + jnp.dot(
            selected_adapter[:, :rank_single],
            adapter_up_weight[adapter_number, :, 0, :],
            preferred_element_type=jnp.float32,
        )
        term_up = term_up + jnp.dot(
            selected_adapter[:, rank_single:],
            adapter_up_weight[adapter_number, :, 1, :],
            preferred_element_type=jnp.float32,
        )
    delta = jnp.concatenate([term_gate.astype(jnp.bfloat16), term_up.astype(jnp.bfloat16)], axis=1)
    spread = lax.all_to_all(requests, "dp", split_axis=1, concat_axis=0, tiled=True)
    weight_flat = base_gate_up_weight.reshape(base_gate_up_weight.shape[0], 2 * rank_extent)
    term = jnp.dot(spread, weight_flat, preferred_element_type=jnp.float32)
    summed = lax.psum_scatter(term, "dp", scatter_dimension=0, tiled=True)
    back = lax.all_to_all(delta, "dp", split_axis=0, concat_axis=0, tiled=True)
    summed = summed + jnp.dot(select_bf.T, back, preferred_element_type=jnp.float32)
    gate = summed[:, :rank_extent]
    up = summed[:, rank_extent:]
    live = row_index < counts[group]
    hidden = jnp.where(live[:, None], jax.nn.silu(gate) * up, 0.0)
    return hidden.astype(jnp.bfloat16)


def solution(mesh):
    placed = (
        P("dp", None),
        P("dp", None, "tensor"),
        P("dp", "tensor", None),
        P("dp", None, None, "tensor"),
        P("dp"),
        P(),
        P(),
    )
    return jax.shard_map(
        body, mesh=mesh, in_specs=placed, out_specs=P("dp", "tensor"), check_vma=False
    )
```

profile of v0, /device:TPU:1, one launch (start us, length us, event | category | flops | bytes accessed | tf_op | source)
XLA Modules:
  0.0 390.8 jit_solution(1881439249161548856)
XLA Ops:
  6.5 2.3 copy.130
  8.9 7.8 %all-to-all-start = ((bf16[64,16,512]{2,0,1:T(8,128)(2,1)}), bf16[64,16,512]{2,0,1:T(8,128)(2,1)S(1)}, u32[]{:S(2)}, u32[]{:S(2)}) async-start(bf16[64,16,512]{2,0,1:T(8,128)(2,1)} %bitcast.132), calls=%async_computation | async-start | bytes 2097152 | tf_op jit(solution)/shard_map/all_to_all | solution.py:81
  16.7 7.8 %copy.96 = bf16[64,8,2,3584]{3,1,2,0:T(8,128)(2,1)} copy(bf16[64,8,2,3584]{3,2,1,0:T(2,128)(2,1)} %bitcast.133) | data formatting | bytes 14680064
  24.6 8.0 %all-to-all-done = bf16[64,16,512]{2,0,1:T(8,128)(2,1)S(1)} async-done(((bf16[64,16,512]{2,0,1:T(8,128)(2,1)}), bf16[64,16,512]{2,0,1:T(8,128)(2,1)S(1)}, u32[]{:S(2)}, u32[]{:S(2)}) %all-to-all-start) | async-done | bytes 1048608 | tf_op jit(solution)/shard_map/all_to_all | solution.py:81
  32.5 16.6 %fusion.87 = f32[1024,7168]{1,0:T(8,128)} fusion(bf16[1024,512]{1,0:T(8,128)(2,1)S(1)} %bitcast.136, bf16[512,7168]{1,0:T(8,128)(2,1)} %bitcast.134), kind=kOutput, calls=%fused_computation.168 | convolution fusion | flops 7516192768 | bytes 37748736 | tf_op jit(solution)/shard_map/dot_general | solution.py:83
  51.3 4.2 %all-to-all-start.1 = ((bf16[16,8,2]{1,2,0:T(2,128)(2,1)}), bf16[16,8,2]{1,2,0:T(2,128)(2,1)S(1)}, u32[]{:S(2)}, u32[]{:S(2)}) async-start(bf16[16,8,2]{1,2,0:T(2,128)(2,1)} %copy.61), calls=%async_computation.2 | async-start | bytes 16384 | tf_op jit(solution)/shard_map/all_to_all | solution.py:52
  55.5 1.9 fusion.3
  57.4 3.6 all-to-all-done.1
  61.0 3.8 all-to-all-start.2
  64.9 17.5 %fusion.86 = (bf16[1,64,1,3584]{3,2,1,0:T(2,128)(2,1)S(1)}, bf16[1,64,1,3584]{3,2,1,0:T(2,128)(2,1)}, bf16[1,64,1,3584]{3,2,1,0:T(2,128)(2,1)}, bf16[1,64,1,3584...) fusion(bf16[8,64,2,3584]{3,2,1,0:T(2,128)(2,1)} %param.10), kind=kLoop, calls=%fused_computation.167 | loop fusion | bytes 14680064 | tf_op jit(solution)/shard_map/slice | solution.py:72
  83.3 1.4 fusion.22
  84.7 1.2 convolution_add_fusion.21
  86.0 1.2 convolution_add_fusion.20
  88.6 35.6 %psum.7 = bf16[128,128]{1,0:T(8,128)(2,1)S(1)} all-reduce(f32[128,128]{1,0:T(8,128)S(1)} %convolution_add_fusion.15), channel_id=1, replica_groups=mesh['dp'=16,'tensor'=8] {'tensor'}, use_global_device_ids=true, to_apply=%region_6.7 | all-reduce | flops 16384 | bytes 98304 | tf_op jit(solution)/shard_map/psum | solution.py:65
  124.5 1.7 fusion.6
  127.1 0.8 copy-done.9
  128.3 0.7 copy-done.8
  129.5 0.7 copy-done.7
  130.7 0.7 copy-done.6
  131.8 0.8 copy-done.5
  133.5 0.7 copy-done.4
  134.6 0.8 copy-done.3
  135.8 0.8 copy-done.2
  137.0 0.8 copy-done.1
  138.2 0.8 copy-done
  140.1 1.4 maximum_bitcast_fusion
  141.6 12.5 %all-to-all-start.3 = ((bf16[16,8,7168]{2,1,0:T(8,128)(2,1)}), bf16[16,8,7168]{2,1,0:T(8,128)(2,1)S(1)}, u32[]{:S(2)}, u32[]{:S(2)}) async-start(bf16[16,8,7168]{2,1,0:T(8,128)(2,1)} %maximum_bitcast_fusion), calls=%async_computation.4 | async-start | bytes 3670016 | tf_op jit(solution)/shard_map/all_to_all | solution.py:85
  154.7 0.6 iota_compare_fusion.5
  155.3 43.2 %all-to-all-done.3 = bf16[16,8,7168]{2,1,0:T(8,128)(2,1)S(1)} async-done(((bf16[16,8,7168]{2,1,0:T(8,128)(2,1)}), bf16[16,8,7168]{2,1,0:T(8,128)(2,1)S(1)}, u32[]{:S(2)}, u32[]{:S(2)}) %all-to-all-start.3) | async-done | bytes 1835040 | tf_op jit(solution)/shard_map/all_to_all | solution.py:85
  198.5 182.4 %reduce-scatter.2.cloned.1.call-done = f32[64,7168]{1,0:T(8,128)} async-done(((f32[1024,7168]{1,0:T(8,128)}), f32[64,7168]{1,0:T(8,128)}) %reduce-scatter.2.cloned.1.call-update) | async-done | bytes 1835024 | tf_op jit(solution)/shard_map/reduce_scatter | solution.py:84
  380.9 2.0 convolution_add_fusion
  382.9 1.0 fusion.5
  (71 shorter events, 11.4 us)
Async XLA Ops:
  8.9 23.7 %all-to-all-start = ((bf16[64,16,512]{2,0,1:T(8,128)(2,1)}), bf16[64,16,512]{2,0,1:T(8,128)(2,1)S(1)}, u32[]{:S(2)}, u32[]{:S(2)}) async-start(bf16[64,16,512]{2,0,1:T(8,128)(2,1)} %bitcast.132), calls=%async_computation | async-start | bytes 2097152 | tf_op jit(solution)/shard_map/all_to_all | solution.py:81
  16.7 364.2 %reduce-scatter.2.cloned.1.call-start = ((), (), s32[]{:S(2)}) async-start(), calls=%async_computation.5 | async-start | bytes 31195136 | tf_op jit(solution)/shard_map/reduce_scatter | solution.py:84
  49.2 0.7 copy-start.13
  49.2 0.7 copy-start.14
  51.3 9.7 %all-to-all-start.1 = ((bf16[16,8,2]{1,2,0:T(2,128)(2,1)}), bf16[16,8,2]{1,2,0:T(2,128)(2,1)S(1)}, u32[]{:S(2)}, u32[]{:S(2)}) async-start(bf16[16,8,2]{1,2,0:T(2,128)(2,1)} %copy.61), calls=%async_computation.2 | async-start | bytes 16384 | tf_op jit(solution)/shard_map/all_to_all | solution.py:52
  61.0 22.3 %all-to-all-start.2 = ((bf16[16,8,1024]{2,1,0:T(8,128)(2,1)}), bf16[16,8,1024]{2,1,0:T(8,128)(2,1)S(1)}, u32[]{:S(2)}, u32[]{:S(2)}) async-start(bf16[16,8,1024]{2,1,0:T(8,128)(2,1)} %fusion.3), calls=%async_computation.3 | async-start | bytes 524288 | tf_op jit(solution)/shard_map/all_to_all | solution.py:51
  83.3 3.9 copy-start.12
  124.3 1.9 copy-start.11
  124.5 2.1 copy-start.10
  126.6 1.2 copy-start.9
  127.8 1.2 copy-start.8
  129.0 1.2 copy-start.7
  130.2 1.2 copy-start.6
  131.4 1.2 copy-start.5
  133.0 1.2 copy-start.4
  134.2 1.2 copy-start.3
  135.4 1.2 copy-start.2
  136.6 1.2 copy-start.1
  137.8 1.2 copy-start
  141.6 12.5 %copy-start.15 = (s32[16]{0:T(128)S(1)}, s32[16]{0:T(128)}, u32[]{:S(2)}) copy-start(s32[16]{0:T(128)} %param.13) | copy-start | bytes 196
  141.6 56.9 %all-to-all-start.3 = ((bf16[16,8,7168]{2,1,0:T(8,128)(2,1)}), bf16[16,8,7168]{2,1,0:T(8,128)(2,1)S(1)}, u32[]{:S(2)}, u32[]{:S(2)}) async-start(bf16[16,8,7168]{2,1,0:T(8,128)(2,1)} %maximum_bitcast_fusion), calls=%async_computation.4 | async-start | bytes 3670016 | tf_op jit(solution)/shard_map/all_to_all | solution.py:85
Sparse Core Ops, SparseCore 0:
  49.3 331.5 reduce-scatter.1
where the time goes:
time: 393 us; the launch traced here: 391 us
  waiting for transfers between devices  237 us (60%)
  local copies, waits for them, and re-layouts  38.1 us (10%)
  blocking collectives  35.6 us (9%)
  matrix products  33.6 us (9%)
  starting transfers between devices  28.4 us (7%)
  between operations  13.8 us (4%)
  other arithmetic  4.04 us (1%)
    reduce_scatter x1, waiting for transfers between devices, body(): summed = lax.psum_scatter(term, 'dp', scatter_dimension=0, tiled=True)  182 us
    all_to_all x1, waiting for transfers between devices, body(): back = lax.all_to_all(delta, 'dp', split_axis=0, concat_axis=0, tiled=True)  43.2 us
    psum x1, blocking collectives, body(): down = lax.psum(partial_down, 'tensor').astype(jnp.bfloat16)  35.6 us
    slice x1, local copies, waits for them, and re-layouts, body(): adapter_up_weight[adapter_number, :, 0, :]  17.5 us
    dot_general x1, matrix products, body(): term = jnp.dot(spread, weight_flat, preferred_element_type=jnp.float32)  16.6 us
    unnamed x33, local copies, waits for them, and re-layouts  16.1 us
    all_to_all x1, starting transfers between devices, body(): back = lax.all_to_all(delta, 'dp', split_axis=0, concat_axis=0, tiled=True)  12.5 us
    all_to_all x1, waiting for transfers between devices, body(): lax.all_to_all(requests, 'dp', split_axis=1, concat_axis=0, tiled=True)  7.96 us
  transfers between devices with their start and end apart: 5, of which 4 were waited for; matrix products, arithmetic and copies ran while one was open for 12% of the time, Pallas kernels for 0%

commit v1 on v0

v1 whole, which is shorter than its diff:
```python
import functools

import jax
import jax.numpy as jnp
from jax import lax
from jax.experimental import pallas as pl
from jax.experimental.pallas import tpu as pltpu
from jax.sharding import PartitionSpec as P

MESH = pl.DeviceIdType.MESH
BF = jnp.bfloat16
F32 = jnp.float32
CHUNKS = 7
NA = 4
NB = 3


def remote(src, dst, send, recv, dp, tensor):
    return pltpu.make_async_remote_copy(
        src_ref=src, dst_ref=dst, send_sem=send, recv_sem=recv,
        device_id=(dp, tensor), device_id_type=MESH,
    )


def kernel(
    x, routed, wt, ut, ad, out,
    xe, we, uv, av, arr, dpart, rsr, dfull, rx, dl, part,
    a2s, a2r, a1s, a1r, ays, ayr, bys, byr, b2s, b2r, b1s, b1r, hs, hid,
    loc, ro_s, ro_r, x_s, x_r, xl_s, xl_r, w_s, w_r, t1_s, t1_r, t2_s, t2_r, rx_s, rx_r, dl_s, dl_r,
    a2_s, a2_q, a1_s, a1_q, ay_s, ay_q, by_s, by_q, b2_s, b2_q, b1_s, b1_q, h_s, h_q,
):
    d = lax.axis_index("dp")
    t = lax.axis_index("tensor")
    n_t = lax.axis_size("tensor")
    chip, c = lax.div(d, 2), lax.rem(d, 2)
    z, y = lax.div(chip, 2), lax.rem(chip, 2)
    yo = 1 - y
    mate = chip * 2 + 1 - c
    zp, zm, z2 = lax.rem(z + 1, 4), lax.rem(z + 3, 4), lax.rem(z + 2, 4)
    to_zp = (zp * 2 + y) * 2 + c
    to_zm = (zm * 2 + y) * 2 + c
    to_y = (z * 2 + yo) * 2 + c
    kc = xe.shape[1] - 256
    kh = kc // 2
    cw = we.shape[2]
    hw = cw // 2
    sub = rsr.shape[1]

    own_w = pltpu.make_async_copy(wt.at[c], we.at[:, pl.ds(c * kh, kh), :], loc.at[0])
    own_u = pltpu.make_async_copy(ut, uv, loc.at[1])
    own_a = pltpu.make_async_copy(ad, av, loc.at[2])
    own_r = pltpu.make_async_copy(routed.at[d], arr.at[d], loc.at[3])
    x_mine = x.at[:, pl.ds(pl.multiple_of(chip * kc, 128), kc)]
    x_rows = xe.at[pl.ds(d * 64, 64), pl.ds(0, kc)]
    own_x = pltpu.make_async_copy(x_mine, x_rows, loc.at[4])
    own_r.start()
    own_a.start()
    own_x.start()
    own_w.start()
    own_u.start()

    barrier = pltpu.get_barrier_semaphore()

    @pl.loop(1, 16)
    def _(i):
        pl.semaphore_signal(barrier, inc=1, device_id=(lax.rem(d + i, 16), t), device_id_type=MESH)

    @pl.loop(1, n_t)
    def _(i):
        pl.semaphore_signal(barrier, inc=1, device_id=(d, lax.rem(t + i, n_t)), device_id_type=MESH)

    pl.semaphore_wait(barrier, 15 + n_t - 1)

    def routed_copy(i):
        peer = lax.rem(d + i, 16)
        return remote(routed.at[peer], arr.at[d], ro_s.at[i], ro_r.at[i], peer, t)

    def x_copy(i):
        q = lax.rem(chip + i, 8)
        src = x.at[:, pl.ds(pl.multiple_of(q * kc, 128), kc)]
        return remote(src, x_rows, x_s.at[i], x_r.at[i], q * 2 + c, t)

    def x_relay(i):
        block = (lax.rem(chip + 8 - i, 8)) * 2 + c
        rows = xe.at[pl.ds(block * 64, 64), pl.ds(0, kc)]
        return remote(rows, rows, xl_s.at[i], xl_r.at[i], mate, t)

    @pl.loop(1, 16)
    def _(i):
        routed_copy(i).start()

    @pl.loop(1, 8)
    def _(i):
        x_copy(i).start()

    x_own_mate = remote(x_mine, x_rows, xl_s.at[0], xl_r.at[0], mate, t)
    x_own_mate.start()
    w_mate = remote(wt.at[1 - c], we.at[:, pl.ds(c * kh, kh), :], w_s, w_r, mate, t)
    w_mate.start()

    own_r.wait()
    own_a.wait()

    @pl.loop(1, 16)
    def _(i):
        routed_copy(i).wait_recv()

    kt = av.shape[1]
    rows_in = arr[...].astype(F32).reshape(128, kt + 128)
    body_in = rows_in[:, :kt].astype(BF)
    lab = rows_in[:, kt:]
    which = lab[:, 0:1].astype(jnp.int32)
    down = jnp.zeros((128, 128), F32)
    for a in range(8):
        term = jnp.dot(body_in, av[a], preferred_element_type=F32)
        down = down + jnp.where(which == a, term, 0.0)
    dpart[...] = down.reshape(n_t, sub, 128)

    def t1_copy(i):
        peer = lax.rem(t + i, n_t)
        return remote(dpart.at[peer], rsr.at[i], t1_s.at[i], t1_r.at[i], d, peer)

    def t2_copy(i):
        peer = lax.rem(t + i, n_t)
        return remote(dfull.at[t], dfull.at[t], t2_s.at[i], t2_r.at[i], d, peer)

    @pl.loop(1, n_t)
    def _(i):
        t1_copy(i).start()

    pick = (lax.broadcasted_iota(jnp.int32, (8, 128), 1) == 1).astype(BF)
    rx[c] = lax.dot_general(
        pick, lab.astype(BF), (((1,), (1,)), ((), ())), preferred_element_type=F32
    )
    rx_copy = remote(rx.at[c], rx.at[c], rx_s, rx_r, mate, t)
    rx_copy.start()

    total = dpart[t]

    @pl.loop(1, n_t)
    def _(i):
        t1_copy(i).wait_recv()

    for i in range(1, n_t):
        total = total + rsr[i]
    dfull[t] = total.astype(BF)

    @pl.loop(1, n_t)
    def _(i):
        t2_copy(i).start()

    @pl.loop(1, 8)
    def _(i):
        x_copy(i).wait_recv()
        x_relay(i).start()

    @pl.loop(1, n_t)
    def _(i):
        t2_copy(i).wait_recv()

    downs = dfull[...].astype(F32).reshape(128, 128).astype(BF)
    lane = lax.broadcasted_iota(jnp.int32, (128, 512), 1)
    src = lax.broadcasted_iota(jnp.int32, (128, 512), 0)
    mine = lax.div(lane, 64) == which

    def spread(offset):
        pattern = (src == lax.rem(lane, 64) + offset).astype(BF)
        copies = jnp.dot(downs, pattern, preferred_element_type=F32)
        return jnp.where(mine, copies, 0.0).astype(BF)

    wide_gate, wide_up = spread(0), spread(64)
    own_u.wait()
    for h in range(2):
        @pl.loop(0, CHUNKS)
        def _(j):
            dl[h, j, :, 0:hw] = jnp.dot(
                wide_gate, uv[h, j, :, 0:hw], preferred_element_type=F32
            ).astype(BF)
            dl[h, j, :, hw:cw] = jnp.dot(
                wide_up, uv[h, j, :, hw:cw], preferred_element_type=F32
            ).astype(BF)

    dl_copy = remote(
        dl.at[1 - c], we.at[:, pl.ds(kc + c * 128, 128), :], dl_s, dl_r, mate, t
    )
    dl_copy.start()

    @pl.loop(0, CHUNKS)
    def _(j):
        we[j, pl.ds(pl.multiple_of(kc + c * 128, 128), 128), :] = dl[c, j]

    rx_copy.wait_recv()
    for core in range(2):
        target = lax.broadcasted_iota(jnp.int32, (1024, 128), 1) // 8 * 64 + rx[core][0:1, :].astype(jnp.int32)
        hot = lax.broadcasted_iota(jnp.int32, (1024, 128), 0) == target
        xe[:, kc + core * 128 : kc + core * 128 + 128] = hot.astype(F32).astype(BF)

    own_x.wait()
    own_w.wait()
    x_own_mate.wait_recv()

    @pl.loop(1, 8)
    def _(i):
        x_relay(i).wait_recv()

    w_mate.wait_recv()
    dl_copy.wait_recv()

    def compute(k, first, count):
        @pl.loop(0, count)
        def _(i):
            zz = lax.rem(z + first + i, 4)
            rows = pl.ds(pl.multiple_of(zz * 256, 256), 256)
            part[k, rows, :] = jnp.dot(xe[rows, :], we[k], preferred_element_type=F32)

    def rows_of(zz, yy):
        return pl.ds(pl.multiple_of(zz * 256 + yy * 128, 128), 128)

    def half_of(zz, yy, cc):
        return pl.ds(pl.multiple_of(zz * 256 + yy * 128 + cc * 64, 64), 64)

    def ra2(s, w):
        return remote(a2s.at[s, w], a2r.at[s, w], a2_s.at[s, w], a2_q.at[s, w], (to_zp, to_zm)[w], t)

    def ra1(s, w, p):
        return remote(a1s.at[s, w, p], a1r.at[s, w, p], a1_s.at[s, w, p], a1_q.at[s, w, p], (to_zp, to_zm)[w], t)

    def ray(s):
        return remote(ays.at[s], ayr.at[s], ay_s.at[s], ay_q.at[s], to_y, t)

    def rby(s, i):
        return remote(bys.at[s, i], byr.at[s, i], by_s.at[s, i], by_q.at[s, i], to_y, t)

    def rb2(s, w):
        return remote(b2s.at[s, w], b2r.at[s, w], b2_s.at[s, w], b2_q.at[s, w], (to_zp, to_zm)[w], t)

    def rb1(s, w, p):
        return remote(b1s.at[s, w, p], b1r.at[s, w, p], b1_s.at[s, w, p], b1_q.at[s, w, p], (to_zp, to_zm)[w], t)

    def rh(k):
        return remote(
            hs.at[k, 1 - c], hid.at[c, :, pl.ds(pl.multiple_of(k * hw, 128), hw)],
            h_s.at[k], h_q.at[k], mate, t,
        )

    def a_first(s):
        k = 2 * s
        compute(k, 1, 3)
        a2s[s, 0] = part[k, rows_of(z2, 0), :].astype(BF)
        ra2(s, 0).start()
        a2s[s, 1] = part[k, rows_of(z2, 1), :].astype(BF)
        ra2(s, 1).start()
        a1s[s, 0, 1] = part[k, rows_of(zp, 1), :].astype(BF)
        ra1(s, 0, 1).start()
        a1s[s, 1, 1] = part[k, rows_of(zm, 0), :].astype(BF)
        ra1(s, 1, 1).start()

    def a_pass(s):
        k = 2 * s
        for w, zz in ((0, zp), (1, zm)):
            ra2(s, w).wait_recv()
            a1s[s, w, 0] = (part[k, rows_of(zz, w), :] + a2r[s, w].astype(F32)).astype(BF)
            ra1(s, w, 0).start()

    def a_cross(s):
        k = 2 * s
        compute(k, 0, 1)
        for w in range(2):
            for p in range(2):
                ra1(s, w, p).wait_recv()
        ays[s] = (
            part[k, rows_of(z, yo), :] + a1r[s, yo, 0].astype(F32) + a1r[s, y, 1].astype(F32)
        ).astype(BF)
        ray(s).start()
        part[k, rows_of(z, y), :] = (
            part[k, rows_of(z, y), :] + a1r[s, y, 0].astype(F32) + a1r[s, yo, 1].astype(F32)
        )

    def finish(k, cc, total):
        gate, up = total[:, :hw], total[:, hw:]
        hs[k, cc] = (gate / (1.0 + jnp.exp(-gate)) * up).astype(BF)

    def deliver(k):
        rh(k).start()
        hid[c, :, pl.ds(pl.multiple_of(k * hw, 128), hw)] = hs[k, c]

    def a_last(s):
        k = 2 * s
        ray(s).wait_recv()
        for cc in range(2):
            finish(k, cc, part[k, half_of(z, y, cc), :] + ayr[s, cc * 64 : cc * 64 + 64, :].astype(F32))
        deliver(k)

    def b_first(s):
        k = 2 * s + 1
        compute(k, 0, 4)
        for i in (2, 1, 3, 0):
            zz = lax.rem(z + i, 4)
            bys[s, i] = part[k, rows_of(zz, yo), :].astype(BF)
            rby(s, i).start()

    def b_second(s):
        k = 2 * s + 1
        rby(s, 2).wait_recv()
        for cc in range(2):
            b2s[s, cc] = (
                part[k, half_of(z2, y, cc), :] + byr[s, 2, cc * 64 : cc * 64 + 64, :].astype(F32)
            ).astype(BF)
            rb2(s, cc).start()
        for w, zz, i in ((0, zp, 1), (1, zm, 3)):
            rby(s, i).wait_recv()
            o = 1 - w
            b1s[s, w, 1] = (
                part[k, half_of(zz, y, o), :] + byr[s, i, o * 64 : o * 64 + 64, :].astype(F32)
            ).astype(BF)
            rb1(s, w, 1).start()

    def b_pass(s):
        k = 2 * s + 1
        for w, zz, i in ((0, zp, 1), (1, zm, 3)):
            rb2(s, w).wait_recv()
            b1s[s, w, 0] = (
                part[k, half_of(zz, y, w), :]
                + byr[s, i, w * 64 : w * 64 + 64, :].astype(F32)
                + b2r[s, w].astype(F32)
            ).astype(BF)
            rb1(s, w, 0).start()

    def b_last(s):
        k = 2 * s + 1
        rby(s, 0).wait_recv()
        for w in range(2):
            for p in range(2):
                rb1(s, w, p).wait_recv()
        for cc in range(2):
            finish(
                k, cc,
                part[k, half_of(z, y, cc), :]
                + byr[s, 0, cc * 64 : cc * 64 + 64, :].astype(F32)
                + b1r[s, cc, 0].astype(F32)
                + b1r[s, 1 - cc, 1].astype(F32),
            )
        deliver(k)

    @pl.loop(0, NA)
    def _(s):
        a_first(s)

        @pl.when(s < NB)
        def _():
            b_first(s)

    @pl.loop(0, NA)
    def _(s):
        a_pass(s)

    @pl.loop(0, NA)
    def _(s):
        a_cross(s)

        @pl.when(s < NB)
        def _():
            b_second(s)

    @pl.loop(0, NB)
    def _(s):
        b_pass(s)

    @pl.loop(0, NA)
    def _(s):
        a_last(s)

    @pl.loop(0, NB)
    def _(s):
        b_last(s)

    @pl.loop(0, CHUNKS)
    def _(k):
        rh(k).wait_recv()

    half = hw * CHUNKS
    out[:, 0:half] = hid[0]
    out[:, half : 2 * half] = hid[1]

    @pl.loop(1, 16)
    def _(i):
        routed_copy(i).wait_send()

    @pl.loop(1, 8)
    def _(i):
        x_copy(i).wait_send()
        x_relay(i).wait_send()

    x_own_mate.wait_send()
    w_mate.wait_send()
    rx_copy.wait_send()
    dl_copy.wait_send()

    @pl.loop(1, n_t)
    def _(i):
        t1_copy(i).wait_send()
        t2_copy(i).wait_send()

    @pl.loop(0, NA)
    def _(s):
        ray(s).wait_send()
        for w in range(2):
            ra2(s, w).wait_send()
            for p in range(2):
                ra1(s, w, p).wait_send()

    @pl.loop(0, NB)
    def _(s):
        for i in range(4):
            rby(s, i).wait_send()
        for w in range(2):
            rb2(s, w).wait_send()
            for p in range(2):
                rb1(s, w, p).wait_send()

    @pl.loop(0, CHUNKS)
    def _(k):
        rh(k).wait_send()


def halves(weight, depth, units):
    hw = units // (2 * CHUNKS)
    cut = weight.reshape(depth, 2, 2, CHUNKS, hw)
    return jnp.transpose(cut, (2, 3, 0, 1, 4)).reshape(2, CHUNKS, depth, 2 * hw)


def body(requests, base, adown, aup, request_adapter, adapter_position, counts):
    rows, width = requests.shape
    n_t = lax.axis_size("tensor")
    group, lane = lax.axis_index("dp"), lax.axis_index("tensor")
    units = base.shape[2]
    per_owner, kt, rank2 = adown.shape
    capacity = 8
    slots = 16 * capacity
    match = (
        request_adapter[:, None] == jnp.arange(adapter_position.shape[0], dtype=jnp.int32)[None, :]
    )
    slot = jnp.sum(jnp.where(match, adapter_position[None, :], 0), axis=1)
    owner = slot // per_owner
    local = slot % per_owner
    owner_hot = (owner[:, None] == jnp.arange(16, dtype=jnp.int32)[None, :]).astype(jnp.int32)
    place = jnp.sum(owner_hot * (jnp.cumsum(owner_hot, axis=0) - 1), axis=1)
    target = owner * capacity + place
    select = (target[None, :] == jnp.arange(slots, dtype=jnp.int32)[:, None]).astype(BF)
    piece = lax.dynamic_slice_in_dim(requests, lane * kt, kt, 1)
    row_index = jnp.arange(rows, dtype=jnp.int32)
    lanes = jnp.arange(128, dtype=jnp.int32)[None, :]
    labels = jnp.where(
        lanes == 0, local[:, None], jnp.where(lanes == 1, row_index[:, None], 0)
    ).astype(BF)
    routed = jnp.dot(
        select, jnp.concatenate([piece, labels], axis=1), preferred_element_type=F32
    ).astype(BF).reshape(16, capacity, kt + 128)

    wt = halves(base, base.shape[0], units)
    ut = halves(aup, aup.shape[0] * aup.shape[1], units)
    kc = width // 8
    hw = units // (2 * CHUNKS)
    cw = 2 * hw
    sub = 128 // n_t
    vm, dma = pltpu.VMEM, pltpu.SemaphoreType.DMA
    both = [
        vm((NA, 2, 128, cw), BF), vm((NA, 2, 128, cw), BF),
        vm((NA, 2, 2, 128, cw), BF), vm((NA, 2, 2, 128, cw), BF),
        vm((NA, 128, cw), BF), vm((NA, 128, cw), BF),
        vm((NB, 4, 128, cw), BF), vm((NB, 4, 128, cw), BF),
        vm((NB, 2, 64, cw), BF), vm((NB, 2, 64, cw), BF),
        vm((NB, 2, 2, 64, cw), BF), vm((NB, 2, 2, 64, cw), BF),
        vm((CHUNKS, 2, 64, hw), BF), vm((2, 64, hw * CHUNKS), BF),
    ]
    sems = [
        dma((5,)), dma((16,)), dma((16,)), dma((8,)), dma((8,)), dma((8,)), dma((8,)),
        dma, dma, dma((n_t,)), dma((n_t,)), dma((n_t,)), dma((n_t,)), dma, dma, dma, dma,
        dma((NA, 2)), dma((NA, 2)), dma((NA, 2, 2)), dma((NA, 2, 2)), dma((NA,)), dma((NA,)),
        dma((NB, 4)), dma((NB, 4)), dma((NB, 2)), dma((NB, 2)), dma((NB, 2, 2)), dma((NB, 2, 2)),
        dma((CHUNKS,)), dma((CHUNKS,)),
    ]
    hidden = pl.pallas_call(
        kernel,
        out_shape=jax.ShapeDtypeStruct((rows, units), BF),
        in_specs=[pl.BlockSpec(memory_space=pl.ANY)] * 5,
        out_specs=pl.BlockSpec(memory_space=pltpu.VMEM),
        scratch_shapes=[
            vm((16 * rows, kc + 256), BF), vm((CHUNKS, kc + 256, cw), BF),
            vm(ut.shape, BF), vm(adown.shape, BF), vm((16, capacity, kt + 128), BF),
            vm((n_t, sub, 128), F32), vm((n_t, sub, 128), F32), vm((n_t, sub, 128), BF),
            vm((2, 8, 128), F32), vm((2, CHUNKS, 128, cw), BF), vm((CHUNKS, 16 * rows, cw), F32),
        ] + both + sems,
        compiler_params=pltpu.CompilerParams(
            collective_id=0, has_side_effects=True, vmem_limit_bytes=67043328
        ),
    )(requests, routed, wt, ut, adown)
    live = row_index < counts[group]
    return jnp.where(live[:, None], hidden, jnp.zeros_like(hidden))


def solution(mesh):
    placed = (
        P("dp", None),
        P("dp", None, "tensor"),
        P("dp", "tensor", None),
        P("dp", None, None, "tensor"),
        P("dp"),
        P(),
        P(),
    )
    return jax.shard_map(
        body, mesh=mesh, in_specs=placed, out_specs=P("dp", "tensor"), check_vma=False
    )
```

time: 393 us -> 192 us (0.49)
  waiting for transfers between devices: 237 us -> 0 us
  Pallas kernels: 0 us -> 89.4 us
  local copies, waits for them, and re-layouts: 38.1 us -> 95.7 us
  blocking collectives: 35.6 us -> 0 us
  matrix products: 33.6 us -> 0.93 us
  starting transfers between devices: 28.4 us -> 0 us
  between operations: 13.8 us -> 0.06 us
    reduce_scatter x1 -> x0, waiting for transfers between devices: 182 us -> none  [body(): summed = lax.psum_scatter(term, 'dp', scatter_dimension=0, tiled=True)]
    pallas_call x0 -> x1, Pallas kernels: none -> 89.4 us  [body(): pl.pallas_call(kernel, out_shape=jax.ShapeDtypeStruct((rows, units), BF),...]
    all_to_all x4 -> x0, waiting for transfers between devices: 54.7 us -> none  [the longest x1 43.2 us: body(): back = lax.all_to_all(delta, 'dp', split_axis=0, concat_axis=0, tiled=True)]
    reshape x0 -> x3, local copies, waits for them, and re-layouts: none -> 42.9 us  [the longest x2 24.8 us: halves(): return jnp.transpose(cut, (2, 3, 0, 1, 4)).reshape(2, CHUNKS, depth, 2 * hw)]
    psum x1 -> x0, blocking collectives: 35.6 us -> none  [body(): down = lax.psum(partial_down, 'tensor').astype(jnp.bfloat16)]
    dot_general x27 -> x1, matrix products: 33.6 us -> 0.93 us  [body(): jnp.dot(select, jnp.concatenate([piece, labels], axis=1), preferred_eleme...]
    transpose x0 -> x2, local copies, waits for them, and re-layouts: none -> 32.1 us  [halves(): return jnp.transpose(cut, (2, 3, 0, 1, 4)).reshape(2, CHUNKS, depth, 2 * hw)]
    all_to_all x4 -> x0, starting transfers between devices: 28.3 us -> none  [the longest x1 12.5 us: body(): back = lax.all_to_all(delta, 'dp', split_axis=0, concat_axis=0, tiled=True)]
  transfers between devices with their start and end apart: 5 -> 0, of which waited for: 4 -> 0; matrix products, arithmetic and copies ran while one was open for 12% -> 0% of each run, Pallas kernels for 0% -> 0%
where the time goes in v1:
time: 192 us; the launch traced here: 190 us
  local copies, waits for them, and re-layouts  95.7 us (50%)
  Pallas kernels  89.4 us (47%)
  other arithmetic  3.84 us (2%)
    pallas_call x1, Pallas kernels, body(): pl.pallas_call(kernel, out_shape=jax.ShapeDtypeStruct((rows, units), BF),...  89.4 us
    transpose x2, local copies, waits for them, and re-layouts, halves(): return jnp.transpose(cut, (2, 3, 0, 1, 4)).reshape(2, CHUNKS, depth, 2 * hw)  32.1 us
    reshape x2, local copies, waits for them, and re-layouts, halves(): return jnp.transpose(cut, (2, 3, 0, 1, 4)).reshape(2, CHUNKS, depth, 2 * hw)  24.8 us
    unnamed x1, local copies, waits for them, and re-layouts  18.6 us
    reshape x1, local copies, waits for them, and re-layouts, halves(): cut = weight.reshape(depth, 2, 2, CHUNKS, hw)  18.1 us

profile of v1, /device:TPU:1, one launch (start us, length us, event | category | flops | bytes accessed | tf_op | source)
XLA Modules:
  0.0 189.9 jit_solution(3624352771809254623)
XLA Ops:
  0.0 0.9 constant_dynamic-slice_fusion
  0.9 0.8 select_reduce_fusion.1
  1.8 0.1 fusion.5
  1.9 0.1 reduce_window_sum.11
  2.0 0.2 select_reduce_fusion
  2.2 0.1 select_convert_fusion
  2.2 0.9 fusion.routed
  3.2 18.1 %reshape.87 = bf16[512,2,2,7,256]{4,3,2,1,0:T(8,128)(2,1)} reshape(bf16[8,64,2,3584]{3,2,1,0:T(2,128)(2,1)} %param.10) | data formatting | bytes 14680064 | tf_op jit(solution)/shard_map/reshape | solution.py:428
  21.3 13.4 %copy.13 = bf16[2,7,512,2,256]{4,3,2,1,0:T(2,128)(2,1)} copy(bf16[2,7,512,2,256]{4,1,0,3,2:T(8,128)(2,1)} %bitcast.8) | data formatting | bytes 14680064 | tf_op jit(solution)/shard_map/transpose | solution.py:429
  34.6 12.4 %reshape.86.ut = bf16[2,7,512,512]{3,2,1,0:T(8,128)(2,1)} reshape(bf16[2,7,512,2,256]{4,3,2,1,0:T(2,128)(2,1)} %copy.13) | data formatting | bytes 14680064 | tf_op jit(solution)/shard_map/reshape | solution.py:429
  47.1 18.6 %copy.10 = bf16[512,2,3584]{0,2,1:T(8,128)(2,1)} copy(bf16[512,2,3584]{2,1,0:T(2,128)(2,1)} %param.8) | data formatting | bytes 14680064 | tf_op args[1]
  65.6 18.7 %copy.11 = bf16[2,7,512,2,256]{4,3,2,1,0:T(2,128)(2,1)} copy(bf16[2,7,512,2,256]{2,4,1,0,3:T(8,128)(2,1)} %bitcast.9) | data formatting | bytes 14680064 | tf_op jit(solution)/shard_map/transpose | solution.py:429
  84.3 12.4 %reshape.84.wt = bf16[2,7,512,512]{3,2,1,0:T(8,128)(2,1)} reshape(bf16[2,7,512,2,256]{4,3,2,1,0:T(2,128)(2,1)} %copy.11) | data formatting | bytes 14680064 | tf_op jit(solution)/shard_map/reshape | solution.py:429
  96.7 89.4 %shard_map.73 = bf16[64,3584]{1,0:T(8,128)(2,1)} custom-call(bf16[64,8192]{1,0:T(8,128)(2,1)} %x.1, bf16[16,8,1152]{2,1,0:T(8,128)(2,1)} %fusion.routed, bf16[2,7,512,512]{3,2,1,0:T(8,128)(2,1)} %reshape.84.wt, bf16[2,7,512,512]{3,2,1,0:T(8,128)(2,1)} %reshape.86.ut, bf16[8,1024,128]{2,1,0:T(8,128)(2,1)} %ad.1), custom_call_target="tpu_custom_call" | custom-call | tf_op jit(solution)/shard_map/pallas_call | solution.py:483
  186.1 1.2 dynamic_slice.6
  187.4 0.6 iota_compare_fusion.6
  188.0 1.9 broadcast_select_fusion
  (3 shorter events, 0.0 us)

commit v2 on v1

--- a/solution.py
+++ b/solution.py
@@ -24,7 +24,7 @@
 
 def kernel(
     x, routed, wt, ut, ad, out,
-    xe, we, uv, av, arr, dpart, rsr, dfull, rx, dl, part,
+    xe, we, wr, ur, av, arr, dpart, rsr, dfull, rx, dl, part,
     a2s, a2r, a1s, a1r, ays, ayr, bys, byr, b2s, b2r, b1s, b1r, hs, hid,
     loc, ro_s, ro_r, x_s, x_r, xl_s, xl_r, w_s, w_r, t1_s, t1_r, t2_s, t2_r, rx_s, rx_r, dl_s, dl_r,
     a2_s, a2_q, a1_s, a1_q, ay_s, ay_q, by_s, by_q, b2_s, b2_q, b1_s, b1_q, h_s, h_q,
@@ -46,8 +46,14 @@
     hw = cw // 2
     sub = rsr.shape[1]
 
-    own_w = pltpu.make_async_copy(wt.at[c], we.at[:, pl.ds(c * kh, kh), :], loc.at[0])
-    own_u = pltpu.make_async_copy(ut, uv, loc.at[1])
+    half = hw * CHUNKS
+
+    def units(h):
+        return pl.ds(pl.multiple_of(h * half, 128), half)
+
+    w_rows = wr.at[pl.ds(c * kh, kh)]
+    own_w = pltpu.make_async_copy(wt.at[:, :, units(c)], w_rows, loc.at[0])
+    own_u = pltpu.make_async_copy(ut, ur, loc.at[1])
     own_a = pltpu.make_async_copy(ad, av, loc.at[2])
     own_r = pltpu.make_async_copy(routed.at[d], arr.at[d], loc.at[3])
     x_mine = x.at[:, pl.ds(pl.multiple_of(chip * kc, 128), kc)]
@@ -95,8 +101,27 @@
 
     x_own_mate = remote(x_mine, x_rows, xl_s.at[0], xl_r.at[0], mate, t)
     x_own_mate.start()
-    w_mate = remote(wt.at[1 - c], we.at[:, pl.ds(c * kh, kh), :], w_s, w_r, mate, t)
+    w_mate = remote(wt.at[:, :, units(1 - c)], w_rows, w_s, w_r, mate, t)
     w_mate.start()
+
+    to = lax.broadcasted_iota(jnp.int32, (256, 256), 0)
+    at = lax.broadcasted_iota(jnp.int32, (256, 256), 1)
+    parting = (at == lax.rem(to, 128) * 2 + lax.div(to, 128)).astype(F32).astype(BF)
+    blocks = kh // 128
+
+    def part_weight(owner):
+        @pl.loop(0, blocks)
+        def _(i):
+            b = owner * blocks + i
+            rows = pl.ds(pl.multiple_of(b * 128, 128), 128)
+            for j in range(CHUNKS):
+                pairs = wr[rows, :, j * hw : j * hw + hw].reshape(256, hw)
+                parted = jnp.dot(parting, pairs, preferred_element_type=F32).astype(BF)
+                we[j, rows, 0:hw] = parted[0:128]
+                we[j, rows, hw:cw] = parted[128:256]
+
+    own_w.wait()
+    part_weight(c)
 
     own_r.wait()
     own_a.wait()
@@ -159,26 +184,28 @@
         t2_copy(i).wait_recv()
 
     downs = dfull[...].astype(F32).reshape(128, 128).astype(BF)
-    lane = lax.broadcasted_iota(jnp.int32, (128, 512), 1)
-    src = lax.broadcasted_iota(jnp.int32, (128, 512), 0)
-    mine = lax.div(lane, 64) == which
-
-    def spread(offset):
-        pattern = (src == lax.rem(lane, 64) + offset).astype(BF)
+    deep = 2 * ur.shape[0]
+    lane = lax.broadcasted_iota(jnp.int32, (128, deep), 1)
+    src = lax.broadcasted_iota(jnp.int32, (128, deep), 0)
+    mine = lax.div(lane, 128) == which
+    rank = lax.div(lax.rem(lane, 128), 2)
+
+    def spread(which_term):
+        pattern = (src == rank + 64 * which_term).astype(F32).astype(BF)
         copies = jnp.dot(downs, pattern, preferred_element_type=F32)
-        return jnp.where(mine, copies, 0.0).astype(BF)
-
-    wide_gate, wide_up = spread(0), spread(64)
+        return jnp.where(mine & (lax.rem(lane, 2) == which_term), copies, 0.0).astype(BF)
+
+    wide = jnp.concatenate([spread(0), spread(1)], axis=0)
     own_u.wait()
     for h in range(2):
         @pl.loop(0, CHUNKS)
         def _(j):
-            dl[h, j, :, 0:hw] = jnp.dot(
-                wide_gate, uv[h, j, :, 0:hw], preferred_element_type=F32
+            cols = pl.ds(pl.multiple_of(h * half + j * hw, 128), hw)
+            both = jnp.dot(
+                wide, ur[:, :, cols].reshape(deep, hw), preferred_element_type=F32
             ).astype(BF)
-            dl[h, j, :, hw:cw] = jnp.dot(
-                wide_up, uv[h, j, :, hw:cw], preferred_element_type=F32
-            ).astype(BF)
+            dl[h, j, :, 0:hw] = both[0:128]
+            dl[h, j, :, hw:cw] = both[128:256]
 
     dl_copy = remote(
         dl.at[1 - c], we.at[:, pl.ds(kc + c * 128, 128), :], dl_s, dl_r, mate, t
@@ -189,6 +216,8 @@
     def _(j):
         we[j, pl.ds(pl.multiple_of(kc + c * 128, 128), 128), :] = dl[c, j]
 
+    w_mate.wait_recv()
+    part_weight(1 - c)
     rx_copy.wait_recv()
     for core in range(2):
         target = lax.broadcasted_iota(jnp.int32, (1024, 128), 1) // 8 * 64 + rx[core][0:1, :].astype(jnp.int32)
@@ -196,14 +225,12 @@
         xe[:, kc + core * 128 : kc + core * 128 + 128] = hot.astype(F32).astype(BF)
 
     own_x.wait()
-    own_w.wait()
     x_own_mate.wait_recv()
 
     @pl.loop(1, 8)
     def _(i):
         x_relay(i).wait_recv()
 
-    w_mate.wait_recv()
     dl_copy.wait_recv()
 
     def compute(k, first, count):
@@ -378,7 +405,6 @@
     def _(k):
         rh(k).wait_recv()
 
-    half = hw * CHUNKS
     out[:, 0:half] = hid[0]
     out[:, half : 2 * half] = hid[1]
 
@@ -421,12 +447,6 @@
     @pl.loop(0, CHUNKS)
     def _(k):
         rh(k).wait_send()
-
-
-def halves(weight, depth, units):
-    hw = units // (2 * CHUNKS)
-    cut = weight.reshape(depth, 2, 2, CHUNKS, hw)
-    return jnp.transpose(cut, (2, 3, 0, 1, 4)).reshape(2, CHUNKS, depth, 2 * hw)
 
 
 def body(requests, base, adown, aup, request_adapter, adapter_position, counts):
@@ -457,8 +477,7 @@
         select, jnp.concatenate([piece, labels], axis=1), preferred_element_type=F32
     ).astype(BF).reshape(16, capacity, kt + 128)
 
-    wt = halves(base, base.shape[0], units)
-    ut = halves(aup, aup.shape[0] * aup.shape[1], units)
+    ut = aup.reshape(aup.shape[0] * aup.shape[1], 2, units)
     kc = width // 8
     hw = units // (2 * CHUNKS)
     cw = 2 * hw
@@ -487,14 +506,14 @@
         out_specs=pl.BlockSpec(memory_space=pltpu.VMEM),
         scratch_shapes=[
             vm((16 * rows, kc + 256), BF), vm((CHUNKS, kc + 256, cw), BF),
-            vm(ut.shape, BF), vm(adown.shape, BF), vm((16, capacity, kt + 128), BF),
+            vm((kc, 2, units // 2), BF), vm(ut.shape, BF), vm(adown.shape, BF), vm((16, capacity, kt + 128), BF),
             vm((n_t, sub, 128), F32), vm((n_t, sub, 128), F32), vm((n_t, sub, 128), BF),
             vm((2, 8, 128), F32), vm((2, CHUNKS, 128, cw), BF), vm((CHUNKS, 16 * rows, cw), F32),
         ] + both + sems,
         compiler_params=pltpu.CompilerParams(
             collective_id=0, has_side_effects=True, vmem_limit_bytes=67043328
         ),
-    )(requests, routed, wt, ut, adown)
+    )(requests, routed, base, ut, adown)
     live = row_index < counts[group]
     return jnp.where(live[:, None], hidden, jnp.zeros_like(hidden))
 

time: 192 us -> 101 us (0.53); the launches traced: 190 us -> 101 us
  local copies, waits for them, and re-layouts: 95.7 us -> 2.16 us
  Pallas kernels: 89.4 us -> 93.8 us
    reshape x3 -> x0, local copies, waits for them, and re-layouts: 42.9 us -> none  [the longest x2 24.8 us: halves(): return jnp.transpose(cut, (2, 3, 0, 1, 4)).reshape(2, CHUNKS, depth, 2 * hw)]
    transpose x2 -> x0, local copies, waits for them, and re-layouts: 32.1 us -> none  [halves(): return jnp.transpose(cut, (2, 3, 0, 1, 4)).reshape(2, CHUNKS, depth, 2 * hw)]
    unnamed x1 -> x0, local copies, waits for them, and re-layouts: 18.6 us -> none
    pallas_call x1, Pallas kernels: 89.4 us -> 93.8 us  [body(): pl.pallas_call(kernel, out_shape=jax.ShapeDtypeStruct((rows, units), BF),...]
where the time goes in v2:
time: 101 us
  Pallas kernels  93.8 us (93%)
  other arithmetic  4.41 us (4%)
  local copies, waits for them, and re-layouts  2.16 us (2%)
    pallas_call x1, Pallas kernels, body(): pl.pallas_call(kernel, out_shape=jax.ShapeDtypeStruct((rows, units), BF),...  93.8 us

profile of v2, /device:TPU:1, one launch (start us, length us, event | category | flops | bytes accessed | tf_op | source)
XLA Modules:
  0.0 101.3 jit_solution(8150502053854531147)
XLA Ops:
  0.0 1.2 %dynamic_slice.6 = s32[1]{0:T(128)} dynamic-slice(s32[16]{0:T(128)} %param.13, s32[]{:T(128)S(6)} %select_n.46), dynamic_slice_sizes={1} | dynamic-slice | bytes 12 | tf_op jit(solution)/shard_map/dynamic_slice | solution.py:517
  1.2 1.2 %iota_compare_fusion.6 = pred[64]{0:T(512)(128)(4,1)} fusion(s32[]{:T(128)} %bitcast), kind=kLoop, calls=%fused_computation.22 | loop fusion | flops 64 | bytes 68 | tf_op jit(solution)/shard_map/lt | solution.py:517
  2.5 0.8 select_reduce_fusion.1
  3.3 0.1 select_convert_fusion
  3.4 0.1 fusion.5
  3.5 0.1 reduce_window_sum.11
  3.6 0.2 select_reduce_fusion
  3.8 0.9 constant_dynamic-slice_fusion
  4.7 0.9 fusion.routed
  5.6 93.8 %shard_map.73 = bf16[64,3584]{1,0:T(8,128)(2,1)} custom-call(bf16[64,8192]{1,0:T(8,128)(2,1)} %x.1, bf16[16,8,1152]{2,1,0:T(8,128)(2,1)} %fusion.routed, bf16[512,2,3584]{2,1,0:T(2,128)(2,1)} %wt.1, bf16[512,2,3584]{2,1,0:T(2,128)(2,1)} %bitcast.4, bf16[8,1024,128]{2,1,0:T(8,128)(2,1)} %ad.1), custom_call_target="tpu_custom_call" | custom-call | tf_op jit(solution)/shard_map/pallas_call | solution.py:502
  99.4 1.9 %broadcast_select_fusion = bf16[64,3584]{1,0:T(8,128)(2,1)} fusion(bf16[64,3584]{1,0:T(8,128)(2,1)} %shard_map.73, pred[64]{0:T(512)(128)(4,1)} %iota_compare_fusion.6), kind=kLoop, calls=%fused_computation.2 | loop fusion | flops 229376 | bytes 917568 | tf_op jit(solution)/shard_map/jit(_where)/select_n | solution.py:518
  (3 shorter events, 0.0 us)

commit v3 on v2

--- a/solution.py
+++ b/solution.py
@@ -23,8 +23,8 @@
 
 
 def kernel(
-    x, routed, wt, ut, ad, out,
-    xe, we, wr, ur, av, arr, dpart, rsr, dfull, rx, dl, part,
+    x, wanted, positions, wt, ut, ad, out,
+    piece, routed, wide, xe, we, wr, ur, av, arr, dpart, rsr, dfull, rx, dl, part,
     a2s, a2r, a1s, a1r, ays, ayr, bys, byr, b2s, b2r, b1s, b1r, hs, hid,
     loc, ro_s, ro_r, x_s, x_r, xl_s, xl_r, w_s, w_r, t1_s, t1_r, t2_s, t2_r, rx_s, rx_r, dl_s, dl_r,
     a2_s, a2_q, a1_s, a1_q, ay_s, ay_q, by_s, by_q, b2_s, b2_q, b1_s, b1_q, h_s, h_q,
@@ -59,7 +59,10 @@
     x_mine = x.at[:, pl.ds(pl.multiple_of(chip * kc, 128), kc)]
     x_rows = xe.at[pl.ds(d * 64, 64), pl.ds(0, kc)]
     own_x = pltpu.make_async_copy(x_mine, x_rows, loc.at[4])
-    own_r.start()
+    own_p = pltpu.make_async_copy(
+        x.at[:, pl.ds(pl.multiple_of(t * av.shape[1], 128), av.shape[1])], piece, loc.at[5]
+    )
+    own_p.start()
     own_a.start()
     own_x.start()
     own_w.start()
@@ -74,6 +77,32 @@
     @pl.loop(1, n_t)
     def _(i):
         pl.semaphore_signal(barrier, inc=1, device_id=(d, lax.rem(t + i, n_t)), device_id_type=MESH)
+
+    rows, kt = piece.shape
+    named = (lax.broadcasted_iota(jnp.int32, (128, rows), 0) == wanted[...]).astype(F32).astype(BF)
+    store = jnp.broadcast_to(positions[...].astype(F32), (8, 128)).astype(BF)
+    slot = jnp.dot(store, named, preferred_element_type=F32)[0:1, :].astype(jnp.int32)
+    owner, local = lax.div(slot, 8), lax.rem(slot, 8)
+    owned = (lax.broadcasted_iota(jnp.int32, (16, rows), 0) == owner).astype(F32)
+    upto = (
+        lax.broadcasted_iota(jnp.int32, (rows, rows), 0) <= lax.broadcasted_iota(jnp.int32, (rows, rows), 1)
+    ).astype(F32).astype(BF)
+    seen = jnp.dot(owned.astype(BF), upto, preferred_element_type=F32)
+    place = jnp.sum(owned * (seen - 1.0), axis=0, keepdims=True).astype(jnp.int32)
+    select = (
+        lax.broadcasted_iota(jnp.int32, (128, rows), 0) == owner * 8 + place
+    ).astype(F32).astype(BF)
+    kind = lax.broadcasted_iota(jnp.int32, (128, rows), 0)
+    index = lax.broadcasted_iota(jnp.int32, (128, rows), 1)
+    labels = jnp.where(kind == 0, local, jnp.where(kind == 1, index, 0)).astype(F32).astype(BF)
+    routed[:, :, kt : kt + 128] = lax.dot_general(
+        select, labels, (((1,), (1,)), ((), ())), preferred_element_type=F32
+    ).reshape(16, 8, 128).astype(BF)
+    own_p.wait()
+    routed[:, :, 0:kt] = jnp.dot(
+        select, piece[...], preferred_element_type=F32
+    ).reshape(16, 8, kt).astype(BF)
+    own_r.start()
 
     pl.semaphore_wait(barrier, 15 + n_t - 1)
 
@@ -130,7 +159,6 @@
     def _(i):
         routed_copy(i).wait_recv()
 
-    kt = av.shape[1]
     rows_in = arr[...].astype(F32).reshape(128, kt + 128)
     body_in = rows_in[:, :kt].astype(BF)
     lab = rows_in[:, kt:]
@@ -179,43 +207,6 @@
         x_copy(i).wait_recv()
         x_relay(i).start()
 
-    @pl.loop(1, n_t)
-    def _(i):
-        t2_copy(i).wait_recv()
-
-    downs = dfull[...].astype(F32).reshape(128, 128).astype(BF)
-    deep = 2 * ur.shape[0]
-    lane = lax.broadcasted_iota(jnp.int32, (128, deep), 1)
-    src = lax.broadcasted_iota(jnp.int32, (128, deep), 0)
-    mine = lax.div(lane, 128) == which
-    rank = lax.div(lax.rem(lane, 128), 2)
-
-    def spread(which_term):
-        pattern = (src == rank + 64 * which_term).astype(F32).astype(BF)
-        copies = jnp.dot(downs, pattern, preferred_element_type=F32)
-        return jnp.where(mine & (lax.rem(lane, 2) == which_term), copies, 0.0).astype(BF)
-
-    wide = jnp.concatenate([spread(0), spread(1)], axis=0)
-    own_u.wait()
-    for h in range(2):
-        @pl.loop(0, CHUNKS)
-        def _(j):
-            cols = pl.ds(pl.multiple_of(h * half + j * hw, 128), hw)
-            both = jnp.dot(
-                wide, ur[:, :, cols].reshape(deep, hw), preferred_element_type=F32
-            ).astype(BF)
-            dl[h, j, :, 0:hw] = both[0:128]
-            dl[h, j, :, hw:cw] = both[128:256]
-
-    dl_copy = remote(
-        dl.at[1 - c], we.at[:, pl.ds(kc + c * 128, 128), :], dl_s, dl_r, mate, t
-    )
-    dl_copy.start()
-
-    @pl.loop(0, CHUNKS)
-    def _(j):
-        we[j, pl.ds(pl.multiple_of(kc + c * 128, 128), 128), :] = dl[c, j]
-
     w_mate.wait_recv()
     part_weight(1 - c)
     rx_copy.wait_recv()
@@ -224,14 +215,52 @@
         hot = lax.broadcasted_iota(jnp.int32, (1024, 128), 0) == target
         xe[:, kc + core * 128 : kc + core * 128 + 128] = hot.astype(F32).astype(BF)
 
+    @pl.loop(1, n_t)
+    def _(i):
+        t2_copy(i).wait_recv()
+
+    downs = dfull[...].astype(F32).reshape(128, 128).astype(BF)
+    deep = 2 * ur.shape[0]
+    lane = lax.broadcasted_iota(jnp.int32, (128, deep), 1)
+    src = lax.broadcasted_iota(jnp.int32, (128, deep), 0)
+    mine = lax.div(lane, 128) == which
+    rank = lax.div(lax.rem(lane, 128), 2)
+
+    def spread(which_term):
+        pattern = (src == rank + 64 * which_term).astype(F32).astype(BF)
+        copies = jnp.dot(downs, pattern, preferred_element_type=F32)
+        return jnp.where(mine & (lax.rem(lane, 2) == which_term), copies, 0.0).astype(BF)
+
+    wide[0:128] = spread(0)
+    wide[128:256] = spread(1)
+    own_u.wait()
+
+    def dl_copy(j):
+        return remote(
+            dl.at[1 - c, j], we.at[j, pl.ds(kc + c * 128, 128), :], dl_s.at[j], dl_r.at[j], mate, t
+        )
+
+    def adapter_terms(j):
+        for h in range(2):
+            cols = pl.ds(pl.multiple_of(h * half + j * hw, 128), hw)
+            both = jnp.dot(
+                wide[...], ur[:, :, cols].reshape(deep, hw), preferred_element_type=F32
+            ).astype(BF)
+            dl[h, j, :, 0:hw] = both[0:128]
+            dl[h, j, :, hw:cw] = both[128:256]
+        dl_copy(j).start()
+        we[j, pl.ds(pl.multiple_of(kc + c * 128, 128), 128), :] = dl[c, j]
+
+    @pl.loop(0, 2)
+    def _(j):
+        adapter_terms(j)
+
     own_x.wait()
     x_own_mate.wait_recv()
 
     @pl.loop(1, 8)
     def _(i):
         x_relay(i).wait_recv()
-
-    dl_copy.wait_recv()
 
     def compute(k, first, count):
         @pl.loop(0, count)
@@ -272,6 +301,7 @@
 
     def a_first(s):
         k = 2 * s
+        dl_copy(k).wait_recv()
         compute(k, 1, 3)
         a2s[s, 0] = part[k, rows_of(z2, 0), :].astype(BF)
         ra2(s, 0).start()
@@ -320,6 +350,7 @@
 
     def b_first(s):
         k = 2 * s + 1
+        dl_copy(k).wait_recv()
         compute(k, 0, 4)
         for i in (2, 1, 3, 0):
             zz = lax.rem(z + i, 4)
@@ -375,7 +406,12 @@
 
         @pl.when(s < NB)
         def _():
+            adapter_terms(2 * s + 2)
             b_first(s)
+
+        @pl.when(s < NB - 1)
+        def _():
+            adapter_terms(2 * s + 3)
 
     @pl.loop(0, NA)
     def _(s):
@@ -420,7 +456,6 @@
     x_own_mate.wait_send()
     w_mate.wait_send()
     rx_copy.wait_send()
-    dl_copy.wait_send()
 
     @pl.loop(1, n_t)
     def _(i):
@@ -447,35 +482,17 @@
     @pl.loop(0, CHUNKS)
     def _(k):
         rh(k).wait_send()
+        dl_copy(k).wait_send()
 
 
 def body(requests, base, adown, aup, request_adapter, adapter_position, counts):
     rows, width = requests.shape
     n_t = lax.axis_size("tensor")
-    group, lane = lax.axis_index("dp"), lax.axis_index("tensor")
+    group = lax.axis_index("dp")
     units = base.shape[2]
     per_owner, kt, rank2 = adown.shape
     capacity = 8
-    slots = 16 * capacity
-    match = (
-        request_adapter[:, None] == jnp.arange(adapter_position.shape[0], dtype=jnp.int32)[None, :]
-    )
-    slot = jnp.sum(jnp.where(match, adapter_position[None, :], 0), axis=1)
-    owner = slot // per_owner
-    local = slot % per_owner
-    owner_hot = (owner[:, None] == jnp.arange(16, dtype=jnp.int32)[None, :]).astype(jnp.int32)
-    place = jnp.sum(owner_hot * (jnp.cumsum(owner_hot, axis=0) - 1), axis=1)
-    target = owner * capacity + place
-    select = (target[None, :] == jnp.arange(slots, dtype=jnp.int32)[:, None]).astype(BF)
-    piece = lax.dynamic_slice_in_dim(requests, lane * kt, kt, 1)
     row_index = jnp.arange(rows, dtype=jnp.int32)
-    lanes = jnp.arange(128, dtype=jnp.int32)[None, :]
-    labels = jnp.where(
-        lanes == 0, local[:, None], jnp.where(lanes == 1, row_index[:, None], 0)
-    ).astype(BF)
-    routed = jnp.dot(
-        select, jnp.concatenate([piece, labels], axis=1), preferred_element_type=F32
-    ).astype(BF).reshape(16, capacity, kt + 128)
 
     ut = aup.reshape(aup.shape[0] * aup.shape[1], 2, units)
     kc = width // 8
@@ -493,8 +510,8 @@
         vm((CHUNKS, 2, 64, hw), BF), vm((2, 64, hw * CHUNKS), BF),
     ]
     sems = [
-        dma((5,)), dma((16,)), dma((16,)), dma((8,)), dma((8,)), dma((8,)), dma((8,)),
-        dma, dma, dma((n_t,)), dma((n_t,)), dma((n_t,)), dma((n_t,)), dma, dma, dma, dma,
+        dma((6,)), dma((16,)), dma((16,)), dma((8,)), dma((8,)), dma((8,)), dma((8,)),
+        dma, dma, dma((n_t,)), dma((n_t,)), dma((n_t,)), dma((n_t,)), dma, dma, dma((CHUNKS,)), dma((CHUNKS,)),
         dma((NA, 2)), dma((NA, 2)), dma((NA, 2, 2)), dma((NA, 2, 2)), dma((NA,)), dma((NA,)),
         dma((NB, 4)), dma((NB, 4)), dma((NB, 2)), dma((NB, 2)), dma((NB, 2, 2)), dma((NB, 2, 2)),
         dma((CHUNKS,)), dma((CHUNKS,)),
@@ -502,9 +519,12 @@
     hidden = pl.pallas_call(
         kernel,
         out_shape=jax.ShapeDtypeStruct((rows, units), BF),
-        in_specs=[pl.BlockSpec(memory_space=pl.ANY)] * 5,
+        in_specs=[pl.BlockSpec(memory_space=pl.ANY)]
+        + [pl.BlockSpec(memory_space=pltpu.VMEM)] * 2
+        + [pl.BlockSpec(memory_space=pl.ANY)] * 3,
         out_specs=pl.BlockSpec(memory_space=pltpu.VMEM),
         scratch_shapes=[
+            vm((rows, kt), BF), vm((16, capacity, kt + 128), BF), vm((256, 2 * ut.shape[0]), BF),
             vm((16 * rows, kc + 256), BF), vm((CHUNKS, kc + 256, cw), BF),
             vm((kc, 2, units // 2), BF), vm(ut.shape, BF), vm(adown.shape, BF), vm((16, capacity, kt + 128), BF),
             vm((n_t, sub, 128), F32), vm((n_t, sub, 128), F32), vm((n_t, sub, 128), BF),
@@ -513,7 +533,7 @@
         compiler_params=pltpu.CompilerParams(
             collective_id=0, has_side_effects=True, vmem_limit_bytes=67043328
         ),
-    )(requests, routed, base, ut, adown)
+    )(requests, request_adapter.reshape(1, rows), adapter_position.reshape(1, -1), base, ut, adown)
     live = row_index < counts[group]
     return jnp.where(live[:, None], hidden, jnp.zeros_like(hidden))
 

time: 101 us -> 92.8 us (0.919)
  Pallas kernels: 93.8 us -> 88.2 us
  other arithmetic: 4.41 us -> 3.11 us
    pallas_call x1, Pallas kernels: 93.8 us -> 88.2 us  [body(): pl.pallas_call(kernel, out_shape=jax.ShapeDtypeStruct((rows, units), BF),...]
    reduce_sum x2 -> x0, other arithmetic: 1.02 us -> none  [the longest x1 0.85 us: body(): slot = jnp.sum(jnp.where(match, adapter_position[None, :], 0), axis=1)]
where the time goes in v3:
time: 92.8 us; the launch traced here: 92.6 us
  Pallas kernels  88.2 us (95%)
  other arithmetic  3.11 us (3%)
  local copies, waits for them, and re-layouts  1.24 us (1%)
    pallas_call x1, Pallas kernels, body(): pl.pallas_call(kernel, out_shape=jax.ShapeDtypeStruct((rows, units), BF),...  88.2 us
    select_n x1, other arithmetic, body(): return jnp.where(live[:, None], hidden, jnp.zeros_like(hidden))  1.89 us

profile of v3, /device:TPU:1, one launch (start us, length us, event | category | flops | bytes accessed | tf_op | source)
XLA Modules:
  0.0 92.6 jit_solution(376401703511675204)
XLA Ops:
  0.0 1.2 %dynamic_slice.3 = s32[1]{0:T(128)} dynamic-slice(s32[16]{0:T(128)} %param.13, s32[]{:T(128)S(6)} %select_n.7), dynamic_slice_sizes={1} | dynamic-slice | bytes 12 | tf_op jit(solution)/shard_map/dynamic_slice | solution.py:537
  1.2 1.2 %iota_compare_fusion = pred[64]{0:T(512)(128)(4,1)} fusion(s32[]{:T(128)} %bitcast), kind=kLoop, calls=%fused_computation.1 | loop fusion | flops 64 | bytes 68 | tf_op jit(solution)/shard_map/lt | solution.py:537
  2.5 88.2 %shard_map.73 = bf16[64,3584]{1,0:T(8,128)(2,1)} custom-call(bf16[64,8192]{1,0:T(8,128)(2,1)} %x.1, s32[1,64]{1,0:T(1,128)} %bitcast.5, s32[1,128]{1,0:T(1,128)} %bitcast.6, bf16[512,2,3584]{2,1,0:T(2,128)(2,1)} %wt.1, bf16[512,2,3584]{2,1,0:T(2,128)(2,1)} %bitcast.4, bf16[8,1024,128]{2,1,0:T(8,128)(2,1)} %ad.1), custom_call_target="tpu_custom_call" | custom-call | tf_op jit(solution)/shard_map/pallas_call | solution.py:519
  90.7 1.9 %broadcast_select_fusion = bf16[64,3584]{1,0:T(8,128)(2,1)} fusion(bf16[64,3584]{1,0:T(8,128)(2,1)} %shard_map.73, pred[64]{0:T(512)(128)(4,1)} %iota_compare_fusion), kind=kLoop, calls=%fused_computation | loop fusion | flops 229376 | bytes 917568 | tf_op jit(solution)/shard_map/jit(_where)/select_n | solution.py:538

commit v4 on v3

--- a/solution.py
+++ b/solution.py
@@ -130,27 +130,35 @@
 
     x_own_mate = remote(x_mine, x_rows, xl_s.at[0], xl_r.at[0], mate, t)
     x_own_mate.start()
-    w_mate = remote(wt.at[:, :, units(1 - c)], w_rows, w_s, w_r, mate, t)
-    w_mate.start()
+
+    def w_copy(j):
+        src = wt.at[:, :, pl.ds(pl.multiple_of((1 - c) * half + j * hw, 128), hw)]
+        dst = wr.at[pl.ds(c * kh, kh), :, pl.ds(pl.multiple_of(j * hw, 128), hw)]
+        return remote(src, dst, w_s.at[j], w_r.at[j], mate, t)
+
+    @pl.loop(0, CHUNKS)
+    def _(j):
+        w_copy(j).start()
 
     to = lax.broadcasted_iota(jnp.int32, (256, 256), 0)
     at = lax.broadcasted_iota(jnp.int32, (256, 256), 1)
     parting = (at == lax.rem(to, 128) * 2 + lax.div(to, 128)).astype(F32).astype(BF)
     blocks = kh // 128
 
-    def part_weight(owner):
+    def part_weight(core, j):
         @pl.loop(0, blocks)
         def _(i):
-            b = owner * blocks + i
-            rows = pl.ds(pl.multiple_of(b * 128, 128), 128)
-            for j in range(CHUNKS):
-                pairs = wr[rows, :, j * hw : j * hw + hw].reshape(256, hw)
-                parted = jnp.dot(parting, pairs, preferred_element_type=F32).astype(BF)
-                we[j, rows, 0:hw] = parted[0:128]
-                we[j, rows, hw:cw] = parted[128:256]
+            rows = pl.ds(pl.multiple_of((core * blocks + i) * 128, 128), 128)
+            pairs = wr[rows, :, pl.ds(pl.multiple_of(j * hw, 128), hw)].reshape(256, hw)
+            parted = jnp.dot(parting, pairs, preferred_element_type=F32).astype(BF)
+            we[j, rows, 0:hw] = parted[0:128]
+            we[j, rows, hw:cw] = parted[128:256]
 
     own_w.wait()
-    part_weight(c)
+
+    @pl.loop(0, 2)
+    def _(j):
+        part_weight(c, j)
 
     own_r.wait()
     own_a.wait()
@@ -207,8 +215,11 @@
         x_copy(i).wait_recv()
         x_relay(i).start()
 
-    w_mate.wait_recv()
-    part_weight(1 - c)
+    @pl.loop(0, 2)
+    def _(j):
+        w_copy(j).wait_recv()
+        part_weight(1 - c, j)
+
     rx_copy.wait_recv()
     for core in range(2):
         target = lax.broadcasted_iota(jnp.int32, (1024, 128), 1) // 8 * 64 + rx[core][0:1, :].astype(jnp.int32)
@@ -250,6 +261,12 @@
             dl[h, j, :, hw:cw] = both[128:256]
         dl_copy(j).start()
         we[j, pl.ds(pl.multiple_of(kc + c * 128, 128), 128), :] = dl[c, j]
+
+    def prepare(j):
+        adapter_terms(j)
+        part_weight(c, j)
+        w_copy(j).wait_recv()
+        part_weight(1 - c, j)
 
     @pl.loop(0, 2)
     def _(j):
@@ -406,12 +423,12 @@
 
         @pl.when(s < NB)
         def _():
-            adapter_terms(2 * s + 2)
             b_first(s)
+            prepare(2 * s + 2)
 
         @pl.when(s < NB - 1)
         def _():
-            adapter_terms(2 * s + 3)
+            prepare(2 * s + 3)
 
     @pl.loop(0, NA)
     def _(s):
@@ -454,7 +471,6 @@
         x_relay(i).wait_send()
 
     x_own_mate.wait_send()
-    w_mate.wait_send()
     rx_copy.wait_send()
 
     @pl.loop(1, n_t)
@@ -483,6 +499,7 @@
     def _(k):
         rh(k).wait_send()
         dl_copy(k).wait_send()
+        w_copy(k).wait_send()
 
 
 def body(requests, base, adown, aup, request_adapter, adapter_position, counts):
@@ -511,7 +528,7 @@
     ]
     sems = [
         dma((6,)), dma((16,)), dma((16,)), dma((8,)), dma((8,)), dma((8,)), dma((8,)),
-        dma, dma, dma((n_t,)), dma((n_t,)), dma((n_t,)), dma((n_t,)), dma, dma, dma((CHUNKS,)), dma((CHUNKS,)),
+        dma((CHUNKS,)), dma((CHUNKS,)), dma((n_t,)), dma((n_t,)), dma((n_t,)), dma((n_t,)), dma, dma, dma((CHUNKS,)), dma((CHUNKS,)),
         dma((NA, 2)), dma((NA, 2)), dma((NA, 2, 2)), dma((NA, 2, 2)), dma((NA,)), dma((NA,)),
         dma((NB, 4)), dma((NB, 4)), dma((NB, 2)), dma((NB, 2)), dma((NB, 2, 2)), dma((NB, 2, 2)),
         dma((CHUNKS,)), dma((CHUNKS,)),

time: 92.8 us -> 97.4 us (1.050)
  Pallas kernels: 88.2 us -> 92.9 us
    pallas_call x1, Pallas kernels: 88.2 us -> 92.9 us  [body(): pl.pallas_call(kernel, out_shape=jax.ShapeDtypeStruct((rows, units), BF),...]
where the time goes in v4:
time: 97.4 us; the launch traced here: 97.2 us
  Pallas kernels  92.9 us (95%)
  other arithmetic  3.11 us (3%)
  local copies, waits for them, and re-layouts  1.24 us (1%)
    pallas_call x1, Pallas kernels, body(): pl.pallas_call(kernel, out_shape=jax.ShapeDtypeStruct((rows, units), BF),...  92.9 us

profile of v4, /device:TPU:1, one launch (start us, length us, event | category | flops | bytes accessed | tf_op | source)
XLA Modules:
  0.0 97.2 jit_solution(18027018797797669072)
XLA Ops:
  0.0 1.2 %dynamic_slice.3 = s32[1]{0:T(128)} dynamic-slice(s32[16]{0:T(128)} %param.13, s32[]{:T(128)S(6)} %select_n.7), dynamic_slice_sizes={1} | dynamic-slice | bytes 12 | tf_op jit(solution)/shard_map/dynamic_slice | solution.py:554
  1.2 1.2 %iota_compare_fusion = pred[64]{0:T(512)(128)(4,1)} fusion(s32[]{:T(128)} %bitcast), kind=kLoop, calls=%fused_computation.1 | loop fusion | flops 64 | bytes 68 | tf_op jit(solution)/shard_map/lt | solution.py:554
  2.5 92.9 %shard_map.73 = bf16[64,3584]{1,0:T(8,128)(2,1)} custom-call(bf16[64,8192]{1,0:T(8,128)(2,1)} %x.1, s32[1,64]{1,0:T(1,128)} %bitcast.5, s32[1,128]{1,0:T(1,128)} %bitcast.6, bf16[512,2,3584]{2,1,0:T(2,128)(2,1)} %wt.1, bf16[512,2,3584]{2,1,0:T(2,128)(2,1)} %bitcast.4, bf16[8,1024,128]{2,1,0:T(8,128)(2,1)} %ad.1), custom_call_target="tpu_custom_call" | custom-call | tf_op jit(solution)/shard_map/pallas_call | solution.py:536
  95.3 1.9 %broadcast_select_fusion = bf16[64,3584]{1,0:T(8,128)(2,1)} fusion(bf16[64,3584]{1,0:T(8,128)(2,1)} %shard_map.73, pred[64]{0:T(512)(128)(4,1)} %iota_compare_fusion), kind=kLoop, calls=%fused_computation | loop fusion | flops 229376 | bytes 917568 | tf_op jit(solution)/shard_map/jit(_where)/select_n | solution.py:555
